TPU v7x, 32 devices: a 4x4x1 block of a 4x4x8 slice. The times are simulated.
32 devices in a mesh: data: 1 (over z), col: 4 (over y), row: 8 (over x, core).
Axes of the slice: x: 4, y: 4, z: 1, core: 2. Of those that a mesh axis runs over, the one named last changes fastest.
The devices are a block of a 4x4x8 slice.
Arguments:
- image: bfloat16 [256, 128, 3], P(('data', 'row'), 'col')
- w_enc1a: bfloat16 [3, 3, 3, 192], replicated
- b_enc1a: float32 [192], replicated
- w_enc1b: bfloat16 [3, 3, 192, 192], replicated
- b_enc1b: float32 [192], replicated
- w_enc2a: bfloat16 [3, 3, 192, 384], replicated
- b_enc2a: float32 [384], replicated
- w_enc2b: bfloat16 [3, 3, 384, 384], replicated
- b_enc2b: float32 [384], replicated
- w_mid_a: bfloat16 [3, 3, 384, 768], replicated
- b_mid_a: float32 [768], replicated
- w_mid_b: bfloat16 [3, 3, 768, 768], replicated
- b_mid_b: float32 [768], replicated
- w_up2: bfloat16 [2, 2, 768, 384], replicated
- w_dec2a: bfloat16 [3, 3, 768, 384], replicated
- b_dec2a: float32 [384], replicated
- w_dec2b: bfloat16 [3, 3, 384, 384], replicated
- b_dec2b: float32 [384], replicated
- w_up1: bfloat16 [2, 2, 384, 192], replicated
- w_dec1a: bfloat16 [3, 3, 384, 192], replicated
- b_dec1a: float32 [192], replicated
- w_dec1b: bfloat16 [3, 3, 192, 192], replicated
- b_dec1b: float32 [192], replicated
- w_head: bfloat16 [192, 6], replicated
- b_head: float32 [6], replicated
Outputs:
- output: float32 [256, 128, 6], P(('data', 'row'), 'col')
All inputs are finite; a program needn't handle non-finite values.
Results may differ from a plain program's by a relative error of at most 0.0159219.
Values are sent between devices in bfloat16 or wider.
A program may use at most 768 MiB of HBM per device.

v0:
```python
import functools

import jax
import jax.numpy as jnp
from jax import lax
from jax.experimental import pallas as pl
from jax.experimental.pallas import tpu as pltpu
from jax.sharding import PartitionSpec as P

MESH = pl.DeviceIdType.MESH
BF = jnp.bfloat16
F32 = jnp.float32
NORTH, SOUTH, WEST, EAST, NW, NE, SW, SE = range(8)
STEP = ((-1, 0), (1, 0), (0, -1), (0, 1), (-1, -1), (-1, 1), (1, -1), (1, 1))
OPPOSITE = (SOUTH, NORTH, EAST, WEST, SE, SW, NE, NW)
WEIGHTS = ("enc1b", "enc2a", "enc2b", "mid_a", "mid_b", "up2", "dec2a", "dec2b", "up1", "dec1a", "dec1b")
BIASES = ("enc1a", "enc1b", "enc2a", "enc2b", "mid_a", "mid_b", "dec2a", "dec2b", "dec1a", "dec1b", "head")
EXCHANGES = (("x", 8, 3), ("a1", 8, 192), ("s1", 8, 192), ("p1", 4, 192), ("a2", 4, 384), ("s2", 4, 384), ("p2", 2, 384),
             ("ma", 2, 768), ("u2", 4, 384), ("e2", 4, 384), ("u1", 8, 192), ("e1", 8, 192))


def turn(value, shift):
    shift = shift % 16
    return value if shift == 0 else pltpu.roll(value, shift, 0)


def body(rows, cols, *refs):
    refs = list(refs)

    def take(count):
        head = refs[:count]
        del refs[:count]
        return head

    x_ref, w_enc1a, w_head = take(3)
    w_hbm = dict(zip(WEIGHTS, take(len(WEIGHTS))))
    bias = dict(zip(BIASES, take(len(BIASES))))
    (y_ref,) = take(1)
    w_vm = dict(zip(WEIGHTS, take(len(WEIGHTS))))
    maps = dict(zip([e[0] for e in EXCHANGES], take(len(EXCHANGES))))
    packs = dict(zip([e[0] for e in EXCHANGES], take(len(EXCHANGES))))
    lands = dict(zip([e[0] for e in EXCHANGES], take(len(EXCHANGES))))
    corners = dict(zip([e[0] for e in EXCHANGES], take(len(EXCHANGES))))
    mb, d2 = take(2)
    w_sem, send_sem, recv_sem = take(3)

    data = lax.axis_index("data")
    row = lax.axis_index("row")
    col = lax.axis_index("col")
    has_n, has_s, has_w, has_e = row > 0, row < rows - 1, col > 0, col < cols - 1
    has = (has_n, has_s, has_w, has_e, has_n & has_w, has_n & has_e, has_s & has_w, has_s & has_e)

    def neighbour(way):
        return (data, col + STEP[way][1], row + STEP[way][0])

    w_copy = {}
    for index, name in enumerate(WEIGHTS):
        w_copy[name] = pltpu.make_async_copy(w_hbm[name], w_vm[name], w_sem.at[index])
        w_copy[name].start()

    barrier = pltpu.get_barrier_semaphore()
    count = jnp.int32(0)
    for way in range(8):
        @pl.when(has[way])
        def _(way=way):
            pl.semaphore_signal(barrier, inc=1, device_id=neighbour(way), device_id_type=MESH)
        count = count + has[way].astype(jnp.int32)
    pl.semaphore_wait(barrier, count)

    sub = lax.broadcasted_iota(jnp.int32, (16, 128), 0)

    def mask(test, channels):
        s = lax.broadcasted_iota(jnp.int32, (16, channels), 0)
        return test(s)

    def copies(name, way):
        index = [e[0] for e in EXCHANGES].index(name)
        side = EXCHANGES[index][1]
        back = OPPOSITE[way]
        if way < 4:
            source, target = packs[name].at[way], lands[name].at[back]
        else:
            i = 1 if STEP[way][0] < 0 else side
            j = 1 if STEP[way][1] < 0 else side
            source, target = maps[name].at[i, j], corners[name].at[back - 4]
        return pltpu.make_async_remote_copy(
            src_ref=source, dst_ref=target, send_sem=send_sem.at[index, way], recv_sem=recv_sem.at[index, back],
            device_id=neighbour(way), device_id_type=MESH)

    def arrival(name, way):
        index = [e[0] for e in EXCHANGES].index(name)
        target = lands[name].at[way] if way < 4 else corners[name].at[way - 4]
        return pltpu.make_async_remote_copy(
            src_ref=target, dst_ref=target, send_sem=send_sem.at[index, way], recv_sem=recv_sem.at[index, way],
            device_id=neighbour(way), device_id_type=MESH)

    def geometry(name):
        entry = EXCHANGES[[e[0] for e in EXCHANGES].index(name)]
        return entry[1], entry[2]

    def load(ref, *at):
        return ref[at].astype(F32)

    def send(name):
        side, channels = geometry(name)
        m = maps[name]
        tiles = max(side // 4, 1)
        for t in range(tiles):
            across = min(side, 4)
            packed = [None] * 4
            for k in range(across):
                e = 4 * t + k
                north = load(m, 1, 1 + e)
                south = load(m, side, 1 + e)
                west = load(m, 1 + e, 1)
                east = load(m, 1 + e, side)
                parts = (turn(north, 4 * k), turn(south, 4 * k - 12), turn(west, k), turn(east, k - 3))
                for way in range(4):
                    if k == 0:
                        packed[way] = parts[way]
                    else:
                        test = (lambda s: s // 4 == k) if way < 2 else (lambda s: s % 4 == k)
                        packed[way] = jnp.where(mask(test, channels), parts[way], packed[way])
            for way in range(4):
                packs[name][way, t] = packed[way].astype(BF)
        for way in range(8):
            @pl.when(has[way])
            def _(way=way):
                copies(name, way).start()

    def receive(name):
        for way in range(8):
            @pl.when(has[way])
            def _(way=way):
                arrival(name, way).wait_recv()
        side, channels = geometry(name)
        m, land, corner = maps[name], lands[name], corners[name]
        zero = jnp.zeros((16, channels), F32)
        top = mask(lambda s: s < 4, channels)
        bottom = mask(lambda s: s >= 12, channels)
        left = mask(lambda s: s % 4 == 0, channels)
        right = mask(lambda s: s % 4 == 3, channels)

        def came(way, tile):
            return jnp.where(has[way], load(land, way, tile), zero)

        def came_corner(way):
            return jnp.where(has[way], load(corner, way - 4), zero)

        last = side - 1
        for e in range(side):
            t, k = e // 4, e % 4
            m[0, 1 + e] = jnp.where(top, turn(came(NORTH, t), -4 * k), turn(load(m, side, 1 + e), 4)).astype(BF)
            m[side + 1, 1 + e] = jnp.where(bottom, turn(came(SOUTH, t), 12 - 4 * k), turn(load(m, 1, 1 + e), -4)).astype(BF)
            m[1 + e, 0] = jnp.where(left, turn(came(WEST, t), -k), turn(load(m, 1 + e, side), 1)).astype(BF)
            m[1 + e, side + 1] = jnp.where(right, turn(came(EAST, t), 3 - k), turn(load(m, 1 + e, 1), -1)).astype(BF)
        t, k = last // 4, last % 4
        own = turn(load(m, side, side), 5)
        value = jnp.where(top, turn(came(NORTH, t), 1 - 4 * k), own)
        value = jnp.where(left, turn(came(WEST, t), 4 - k), value)
        m[0, 0] = jnp.where(top & left, turn(came_corner(NW), 1), value).astype(BF)
        own = turn(load(m, side, 1), 3)
        value = jnp.where(top, turn(came(NORTH, 0), -1), own)
        value = jnp.where(right, turn(came(EAST, t), 7 - k), value)
        m[0, side + 1] = jnp.where(top & right, turn(came_corner(NE), 7), value).astype(BF)
        own = turn(load(m, 1, side), -3)
        value = jnp.where(bottom, turn(came(SOUTH, t), 13 - 4 * k), own)
        value = jnp.where(left, turn(came(WEST, 0), -4), value)
        m[side + 1, 0] = jnp.where(bottom & left, turn(came_corner(SW), 9), value).astype(BF)
        own = turn(load(m, 1, 1), -5)
        value = jnp.where(bottom, turn(came(SOUTH, 0), 11), own)
        value = jnp.where(right, turn(came(EAST, 0), -1), value)
        m[side + 1, side + 1] = jnp.where(bottom & right, turn(came_corner(SE), 15), value).astype(BF)

    def taps(name):
        side, channels = geometry(name)
        m = maps[name]
        return [m[dy:dy + side, dx:dx + side].reshape(side * side * 16, channels) for dy in range(3) for dx in range(3)]

    def conv_sum(sources, weight, depth):
        total = None
        for name, first in sources:
            channels = geometry(name)[1]
            for t, tap in enumerate(taps(name)):
                part = jnp.dot(tap, weight[pl.ds(t * depth + first, channels), :], preferred_element_type=F32)
                total = part if total is None else total + part
        return total

    def act(total, name):
        return jnp.maximum(total + bias[name][...], 0.0).astype(BF)

    def put(name, value):
        side, channels = geometry(name)
        maps[name][1:side + 1, 1:side + 1] = value.reshape(side, side, 16, channels)

    def pool(source, target):
        side, channels = geometry(target)
        a, b = maps[source], maps[target]
        for i in range(side):
            for j in range(side):
                p, q = 1 + 2 * i, 1 + 2 * j
                b[1 + i, 1 + j] = jnp.maximum(jnp.maximum(a[p, q], a[p, q + 1]), jnp.maximum(a[p + 1, q], a[p + 1, q + 1]))

    def up(value, weight, depth, target, side):
        channels = geometry(target)[1]
        for p in range(2):
            for q in range(2):
                w = weight[pl.ds((2 * p + q) * depth, depth), :]
                out = jnp.dot(value, w, preferred_element_type=F32).astype(BF).reshape(side, side, 16, channels)
                for i in range(side):
                    for j in range(side):
                        maps[target][1 + 2 * i + p, 1 + 2 * j + q] = out[i, j]

    maps["x"][1:9, 1:9] = x_ref[...]
    send("x")
    receive("x")
    total = None
    for t, tap in enumerate(taps("x")):
        part = jnp.dot(tap, w_enc1a[t], preferred_element_type=F32)
        total = part if total is None else total + part
    put("a1", act(total, "enc1a"))
    send("a1")
    receive("a1")
    w_copy["enc1b"].wait()
    put("s1", act(conv_sum([("a1", 0)], w_vm["enc1b"], 192), "enc1b"))
    pool("s1", "p1")
    send("p1")
    send("s1")
    receive("p1")
    w_copy["enc2a"].wait()
    put("a2", act(conv_sum([("p1", 0)], w_vm["enc2a"], 192), "enc2a"))
    send("a2")
    receive("a2")
    w_copy["enc2b"].wait()
    put("s2", act(conv_sum([("a2", 0)], w_vm["enc2b"], 384), "enc2b"))
    pool("s2", "p2")
    send("p2")
    send("s2")
    receive("p2")
    w_copy["mid_a"].wait()
    put("ma", act(conv_sum([("p2", 0)], w_vm["mid_a"], 384), "mid_a"))
    send("ma")
    receive("ma")
    w_copy["mid_b"].wait()
    mb[...] = act(conv_sum([("ma", 0)], w_vm["mid_b"], 768), "mid_b")
    w_copy["up2"].wait()
    up(mb[...], w_vm["up2"], 768, "u2", 2)
    send("u2")
    receive("s2")
    receive("u2")
    w_copy["dec2a"].wait()
    put("e2", act(conv_sum([("u2", 0), ("s2", 384)], w_vm["dec2a"], 768), "dec2a"))
    send("e2")
    receive("e2")
    w_copy["dec2b"].wait()
    d2[...] = act(conv_sum([("e2", 0)], w_vm["dec2b"], 384), "dec2b")
    w_copy["up1"].wait()
    up(d2[...], w_vm["up1"], 384, "u1", 4)
    send("u1")
    receive("s1")
    receive("u1")
    w_copy["dec1a"].wait()
    put("e1", act(conv_sum([("u1", 0), ("s1", 192)], w_vm["dec1a"], 384), "dec1a"))
    send("e1")
    receive("e1")
    w_copy["dec1b"].wait()
    d1 = act(conv_sum([("e1", 0)], w_vm["dec1b"], 192), "dec1b")
    y = jnp.dot(d1, w_head[...], preferred_element_type=F32) + bias["head"][...]
    y_ref[...] = y.reshape(y_ref.shape)

    for name, _, _ in EXCHANGES:
        for way in range(8):
            @pl.when(has[way])
            def _(way=way, name=name):
                copies(name, way).wait_send()


def solution(mesh):
    rows = mesh.shape["row"]
    cols = mesh.shape["col"]
    tile_spec = P(("data", "row"), "col", None)

    def device_body(image, *params):
        names = ("w_enc1a", "b_enc1a", "w_enc1b", "b_enc1b", "w_enc2a", "b_enc2a", "w_enc2b", "b_enc2b", "w_mid_a", "b_mid_a",
                 "w_mid_b", "b_mid_b", "w_up2", "w_dec2a", "b_dec2a", "w_dec2b", "b_dec2b", "w_up1", "w_dec1a", "b_dec1a",
                 "w_dec1b", "b_dec1b", "w_head", "b_head")
        p = dict(zip(names, params))
        high, wide, depth = image.shape
        x = image.reshape(4, high // 4, 4, wide // 4, depth).transpose(1, 3, 0, 2, 4).reshape(high // 4, wide // 4, 16, depth)
        weights = [p["w_" + n].reshape(-1, p["w_" + n].shape[-1]) for n in WEIGHTS]
        biases = [p["b_" + n].reshape(1, -1) for n in BIASES]
        vmem = pl.BlockSpec(memory_space=pltpu.VMEM)
        hbm = pl.BlockSpec(memory_space=pl.ANY)
        out_channels = p["w_head"].shape[1]
        scratch = [pltpu.VMEM(w.shape, BF) for w in weights]
        scratch += [pltpu.VMEM((s + 2, s + 2, 16, c), BF) for _, s, c in EXCHANGES]
        scratch += [pltpu.VMEM((4, max(s // 4, 1), 16, c), BF) for _, s, c in EXCHANGES]
        scratch += [pltpu.VMEM((4, max(s // 4, 1), 16, c), BF) for _, s, c in EXCHANGES]
        scratch += [pltpu.VMEM((4, 16, c), BF) for _, s, c in EXCHANGES]
        scratch += [pltpu.VMEM((64, 768), BF), pltpu.VMEM((256, 384), BF)]
        scratch += [pltpu.SemaphoreType.DMA((len(WEIGHTS),)), pltpu.SemaphoreType.DMA((len(EXCHANGES), 8)),
                    pltpu.SemaphoreType.DMA((len(EXCHANGES), 8))]
        y = pl.pallas_call(
            functools.partial(body, rows, cols),
            out_shape=jax.ShapeDtypeStruct((high // 4, wide // 4, 16, out_channels), F32),
            in_specs=[vmem] * 3 + [hbm] * len(weights) + [vmem] * len(biases),
            out_specs=vmem,
            scratch_shapes=scratch,
            compiler_params=pltpu.CompilerParams(collective_id=0, has_side_effects=True, vmem_limit_bytes=62 * 1024 * 1024),
            name="unet",
        )(x, p["w_enc1a"].reshape(9, depth, -1), p["w_head"], *weights, *biases)
        y = y.reshape(high // 4, wide // 4, 4, 4, out_channels).transpose(2, 0, 3, 1, 4)
        return y.reshape(high, wide, out_channels)

    def program(image, *params):
        mapped = jax.shard_map(device_body, mesh=mesh, in_specs=(tile_spec,) + tuple([P()] * len(params)), out_specs=tile_spec, check_vma=False)
        return mapped(image, *params)

    return program
```

profile of v0, /device:TPU:97, one launch (start us, length us, event | category | flops | bytes accessed | tf_op | source)
XLA Modules:
  0.0 86.7 jit_solution(13389382127197696819)
XLA Ops:
  0.0 0.0 copy-start
  0.0 1.4 %reshape.97.refs_16_ = f32[1,384]{1,0:T(1,128)} reshape(f32[384]{0:T(512)} %param.31) | data formatting | bytes 3072 | tf_op jit(solution)/shard_map/reshape | solution.py:291
  1.4 1.3 %reshape.98.refs_17_ = f32[1,384]{1,0:T(1,128)} reshape(f32[384]{0:T(512)} %param.33) | data formatting | bytes 3072 | tf_op jit(solution)/shard_map/reshape | solution.py:291
  2.6 1.3 %reshape.101.refs_20_ = f32[1,384]{1,0:T(1,128)} reshape(f32[384]{0:T(512)} %param.40) | data formatting | bytes 3072 | tf_op jit(solution)/shard_map/reshape | solution.py:291
  3.9 1.3 %reshape.102.refs_21_ = f32[1,384]{1,0:T(1,128)} reshape(f32[384]{0:T(512)} %param.42) | data formatting | bytes 3072 | tf_op jit(solution)/shard_map/reshape | solution.py:291
  5.2 1.3 %reshape.99.refs_18_ = f32[1,768]{1,0:T(1,128)} reshape(f32[768]{0:T(1024)} %param.35) | data formatting | bytes 6144 | tf_op jit(solution)/shard_map/reshape | solution.py:291
  6.5 1.3 %reshape.100.refs_19_ = f32[1,768]{1,0:T(1,128)} reshape(f32[768]{0:T(1024)} %param.37) | data formatting | bytes 6144 | tf_op jit(solution)/shard_map/reshape | solution.py:291
  7.7 1.4 %copy.29.refs_2_ = bf16[192,6]{1,0:T(8,128)(2,1)} copy(bf16[192,6]{0,1:T(8,128)(2,1)} %param.48) | data formatting | bytes 4608 | tf_op args[23]
  9.2 0.8 reshape.81
  10.0 1.6 %copy.26 = bf16[4,8,4,8,3]{4,2,0,3,1:T(4,128)(2,1)} copy(bf16[4,8,4,8,3]{3,2,1,0,4:T(4,128)(2,1)S(1)} %reshape.81) | data formatting | bytes 12288 | tf_op jit(solution)/shard_map/reshape | solution.py:289
  11.6 2.2 %copy.27 = bf16[2,2,384,192]{3,2,1,0:T(8,128)(2,1)} copy(bf16[2,2,384,192]{2,3,1,0:T(8,128)(2,1)} %param.43) | data formatting | bytes 1179648 | tf_op args[18]
  13.8 0.0 copy-done
  13.8 2.2 %copy.28 = bf16[3,3,384,192]{3,2,1,0:T(8,128)(2,1)} copy(bf16[3,3,384,192]{2,3,1,0:T(8,128)(2,1)S(1)} %copy-done) | data formatting | bytes 2654208 | tf_op args[19]
  16.1 67.6 %unet.1 = f32[8,8,16,6]{3,2,1,0:T(8,128)} custom-call(bf16[8,8,16,3]{3,2,1,0:T(8,128)(2,1)} %bitcast.37, bf16[9,3,192]{2,1,0:T(4,128)(2,1)} %bitcast.40, bf16[192,6]{1,0:T(8,128)(2,1)} %copy.29.refs_2_, bf16[1728,192]{1,0:T(8,128)(2,1)} %bitcast.38, bf16[1728,384]{1,0:T(8,128)(2,1)} %bitcast.36, bf16[3456,384]{1,0:T(8,128)(2,1)} %bitcast.32, ...), custom_call_target="tpu_custom_call" | custom-call | tf_op jit(solution)/shard_map/unet/pallas_call | solution.py:303
  83.7 2.2 %copy.30 = f32[4,8,4,8,6]{3,2,1,0,4:T(4,128)S(1)} copy(f32[4,8,4,8,6]{4,2,0,3,1:T(4,128)} %bitcast.35) | data formatting | bytes 49152 | tf_op jit(solution)/shard_map/transpose | solution.py:312
  85.9 0.9 reshape.107
Async XLA Ops:
  0.0 13.8 %copy-start = (bf16[3,3,384,192]{2,3,1,0:T(8,128)(2,1)S(1)}, bf16[3,3,384,192]{2,3,1,0:T(8,128)(2,1)}, u32[]{:S(2)}) copy-start(bf16[3,3,384,192]{2,3,1,0:T(8,128)(2,1)} %param.44) | copy-start | bytes 3981316
where the time goes:
time: 87.1 us; the launch traced here: 86.7 us
  Pallas kernels  67.6 us (78%)
  local copies, waits for them, and re-layouts  19.1 us (22%)
    pallas_call x1, Pallas kernels, device_body(): pl.pallas_call(functools.partial(body, rows, cols), out_shape=jax.ShapeDt...  67.6 us
    reshape x6, local copies, waits for them, and re-layouts, device_body(): biases = [p['b_' + n].reshape(1, -1) for n in BIASES]  7.71 us
    unnamed x5, local copies, waits for them, and re-layouts  5.9 us
    reshape x2, local copies, waits for them, and re-layouts, device_body(): image.reshape(4, high // 4, 4, wide // 4, depth).transpose(1, 3, 0, 2, 4)  2.45 us
    transpose x1, local copies, waits for them, and re-layouts, device_body(): y.reshape(high // 4, wide // 4, 4, 4, out_channels).transpose(2, 0, 3, 1, 4)  2.17 us

commit v1 on v0

v1 whole, which is shorter than its diff:
```python
import functools

import jax
import jax.numpy as jnp
from jax import lax
from jax.experimental import pallas as pl
from jax.experimental.pallas import tpu as pltpu
from jax.sharding import PartitionSpec as P

MESH = pl.DeviceIdType.MESH
BF = jnp.bfloat16
F32 = jnp.float32
STEP = ((-1, 0), (1, 0), (0, -1), (0, 1), (-1, -1), (-1, 1), (1, -1), (1, 1))
OPPOSITE = (1, 0, 3, 2, 7, 6, 5, 4)
WEIGHTS = ("enc1b", "enc2a", "enc2b", "mid_a", "mid_b", "up2", "dec2a", "dec2b", "up1", "dec1a", "dec1b")
TURNED = ("up1", "dec1a")
BIASES = ("enc1a", "enc1b", "enc2a", "enc2b", "mid_a", "mid_b", "dec2a", "dec2b", "dec1a", "dec1b")
MAPS = {"x": (8, 2, 128), "s1": (8, 1, 192), "p1": (4, 2, 192), "s2": (4, 1, 384), "p2": (2, 2, 384), "u2": (4, 1, 384),
        "e2": (4, 1, 384), "u1": (8, 1, 192), "e1": (8, 1, 192), "a1": (8, 1, 192), "a2": (4, 1, 384), "ma": (2, 1, 768)}
SHARED = ("x", "s1", "p1", "s2", "p2", "u2", "e2", "u1", "e1")


def tiles_of(name):
    side, ring, _ = MAPS[name]
    return max(side * ring // 4, 1)


def turn(value, shift):
    shift = shift % 16
    return value if shift == 0 else pltpu.roll(value, shift, 0)


def rows_dot(a, b):
    return lax.dot_general(a, b, (((1,), (1,)), ((), ())), preferred_element_type=F32)


def iota(shape, axis):
    return lax.broadcasted_iota(jnp.int32, shape, axis)


def body(rows, cols, *refs):
    refs = list(refs)

    def take(count):
        head = refs[:count]
        del refs[:count]
        return head

    x_ref, w_enc1a, w_head, b_head = take(4)
    w_hbm = dict(zip(WEIGHTS, take(len(WEIGHTS))))
    bias = dict(zip(BIASES, take(len(BIASES))))
    (y_ref,) = take(1)
    w_vm = dict(zip(WEIGHTS, take(len(WEIGHTS))))
    maps = dict(zip(MAPS, take(len(MAPS))))
    packs = dict(zip(SHARED, take(len(SHARED))))
    lands = dict(zip(SHARED, take(len(SHARED))))
    x27, w27, mb, d2, d1, acc1, acc2, y_rows = take(8)
    w_sem, send_sem, recv_sem = take(3)

    data = lax.axis_index("data")
    row = lax.axis_index("row")
    col = lax.axis_index("col")
    go = row >= 0
    has_n, has_s, has_w, has_e = row > 0, row < rows - 1, col > 0, col < cols - 1
    has = (has_n, has_s, has_w, has_e, has_n & has_w, has_n & has_e, has_s & has_w, has_s & has_e)

    def neighbour(way):
        return (data, col + STEP[way][1], row + STEP[way][0])

    w_copy = {}
    for index, name in enumerate(WEIGHTS):
        w_copy[name] = pltpu.make_async_copy(w_hbm[name], w_vm[name], w_sem.at[index])
        w_copy[name].start()

    barrier = pltpu.get_barrier_semaphore()
    count = jnp.int32(0)
    for way in range(8):
        @pl.when(has[way])
        def _(way=way):
            pl.semaphore_signal(barrier, inc=1, device_id=neighbour(way), device_id_type=MESH)
        count = count + has[way].astype(jnp.int32)

    def land(name, way):
        tiles = tiles_of(name)
        return lands[name].at[pl.ds(way * tiles, tiles)] if way < 4 else lands[name].at[pl.ds(4 * tiles + way - 4, 1)]

    def pack(name, way):
        tiles = tiles_of(name)
        return packs[name].at[pl.ds(way * tiles, tiles)] if way < 4 else packs[name].at[pl.ds(4 * tiles + way - 4, 1)]

    def copies(name, way):
        index = SHARED.index(name)
        back = OPPOSITE[way]
        return pltpu.make_async_remote_copy(
            src_ref=pack(name, way), dst_ref=land(name, back), send_sem=send_sem.at[index, way],
            recv_sem=recv_sem.at[index, back], device_id=neighbour(way), device_id_type=MESH)

    def arrival(name, way):
        index = SHARED.index(name)
        return pltpu.make_async_remote_copy(
            src_ref=pack(name, way), dst_ref=land(name, way), send_sem=send_sem.at[index, way],
            recv_sem=recv_sem.at[index, way], device_id=neighbour(way), device_id_type=MESH)

    def sublane(channels):
        return iota((16, channels), 0)

    def spot(name, way, i, j):
        side, ring, _ = MAPS[name]
        di, dj = STEP[way]
        i = i - (side - ring) if di > 0 else i
        j = j - (side - ring) if dj > 0 else j
        return i * side + j if dj == 0 else i * ring + j

    def span(side, ring, d):
        return range(side) if d == 0 else range(ring) if d < 0 else range(side - ring, side)

    def send(name):
        side, ring, channels = MAPS[name]
        m, tiles = maps[name], tiles_of(name)
        s = sublane(channels)
        for way in range(8):
            di, dj = STEP[way]
            packed = {}
            for i in span(side, ring, di):
                for j in span(side, ring, dj):
                    e = spot(name, way, i, j)
                    value = m[ring + i, ring + j].astype(F32)
                    edge = 4 * (3 if di > 0 else 0) + (3 if dj > 0 else 0)
                    if way < 4:
                        t, k = e // 4, e % 4
                        value = turn(value, (4 * k if dj == 0 else k) - edge)
                        test = (s >> 2) == k if dj == 0 else (s & 3) == k
                    else:
                        t, k = 0, e
                        value = turn(value, k - edge)
                        test = s == k
                    packed[t] = value if t not in packed else jnp.where(test, value, packed[t])
            for t, value in packed.items():
                packs[name][(way * tiles if way < 4 else 4 * tiles + way - 4) + t] = value.astype(BF)
        for way in range(8):
            @pl.when(has[way])
            def _(way=way):
                copies(name, way).start()

    def receive(name):
        for way in range(8):
            @pl.when(has[way])
            def _(way=way):
                arrival(name, way).wait_recv()
        side, ring, channels = MAPS[name]
        m, tiles = maps[name], tiles_of(name)
        s = sublane(channels)
        zero = jnp.zeros((16, channels), F32)

        def came(way, tile):
            value = lands[name][(way * tiles if way < 4 else 4 * tiles + way - 4) + tile].astype(F32)
            return jnp.where(has[way], value, zero)

        for i in range(-ring, side + ring):
            for j in range(-ring, side + ring):
                di = -1 if i < 0 else 1 if i >= side else 0
                dj = -1 if j < 0 else 1 if j >= side else 0
                if di == 0 and dj == 0:
                    continue
                si, sj = i % side, j % side
                value = turn(m[ring + si, ring + sj].astype(F32), -4 * di - dj)
                hb, wb = (3 if di > 0 else 0), (3 if dj > 0 else 0)
                if di:
                    way = STEP.index((di, 0))
                    e = spot(name, OPPOSITE[way], si, sj)
                    value = jnp.where((s >> 2) == hb, turn(came(way, e // 4), 4 * hb - 4 * (e % 4) - dj), value)
                if dj:
                    way = STEP.index((0, dj))
                    e = spot(name, OPPOSITE[way], si, sj)
                    value = jnp.where((s & 3) == wb, turn(came(way, e // 4), wb - 4 * di - e % 4), value)
                if di and dj:
                    way = STEP.index((di, dj))
                    e = spot(name, OPPOSITE[way], si, sj)
                    value = jnp.where(s == 4 * hb + wb, turn(came(way, 0), 4 * hb + wb - e), value)
                m[ring + i, ring + j] = value.astype(BF)

    def clear_outside(name):
        side, ring, channels = MAPS[name]
        m = maps[name]
        s = sublane(channels)
        zero = jnp.zeros((16, channels), F32)
        inside = [None] * 4
        for way, test in enumerate(((s >> 2) == 0, (s >> 2) == 3, (s & 3) == 0, (s & 3) == 3)):
            inside[way] = jnp.logical_or(jnp.logical_not(test), has[way])
        for i in range(-ring, side + ring):
            for j in range(-ring, side + ring):
                ways = [w for w, out in enumerate((i < 0, i >= side, j < 0, j >= side)) if out]
                if ways:
                    value = m[ring + i, ring + j].astype(F32)
                    for way in ways:
                        value = jnp.where(inside[way], value, zero)
                    m[ring + i, ring + j] = value.astype(BF)

    def taps(name, out_ring):
        side, ring, channels = MAPS[name]
        m, first, size = maps[name], ring - 1 - out_ring, side + 2 * out_ring
        return [m[first + dy:first + dy + size, first + dx:first + dx + size].reshape(size * size * 16, channels)
                for dy in range(3) for dx in range(3)]

    def conv_sum(name, weight, first, depth, out_ring=0):
        total = None
        channels = MAPS[name][2]
        for t, tap in enumerate(taps(name, out_ring)):
            if weight in TURNED:
                part = rows_dot(tap, w_vm[weight][pl.ds(t * 192, 192), first:first + channels])
            else:
                part = jnp.dot(tap, w_vm[weight][pl.ds(t * depth + first, channels), :], preferred_element_type=F32)
            total = part if total is None else total + part
        return total

    def act(total, name):
        return jnp.maximum(total + bias[name][...][None, :], 0.0).astype(BF)

    def put(name, value, out_ring=0):
        side, ring, channels = MAPS[name]
        size, first = side + 2 * out_ring, ring - out_ring
        maps[name][first:first + size, first:first + size] = value.reshape(size, size, 16, channels)

    def layer(target, source, weight, depth, out_ring=0):
        w_copy[weight].wait()

        @pl.when(go)
        def _():
            put(target, act(conv_sum(source, weight, 0, depth, out_ring), weight), out_ring)

    def pool(source, target):
        side, ring, channels = MAPS[target]
        a, b, first = maps[source], maps[target], MAPS[source][1]
        for i in range(side):
            for j in range(side):
                p, q = first + 2 * i, first + 2 * j
                b[ring + i, ring + j] = jnp.maximum(jnp.maximum(a[p, q], a[p, q + 1]), jnp.maximum(a[p + 1, q], a[p + 1, q + 1]))

    def up(value, weight, target):
        side, ring, channels = MAPS[target]
        depth = value.shape[1]
        w_copy[weight].wait()

        @pl.when(go)
        def _():
            for p in range(2):
                for q in range(2):
                    if weight in TURNED:
                        out = rows_dot(value[...], w_vm[weight][pl.ds((2 * p + q) * channels, channels), :])
                    else:
                        out = jnp.dot(value[...], w_vm[weight][pl.ds((2 * p + q) * depth, depth), :], preferred_element_type=F32)
                    out = out.astype(BF).reshape(side // 2, side // 2, 16, channels)
                    for i in range(side // 2):
                        for j in range(side // 2):
                            maps[target][ring + 2 * i + p, ring + 2 * j + q] = out[i, j]

    lane, low = iota((32, 128), 1), iota((32, 128), 0)
    pixels = x_ref[...].astype(F32)
    z = None
    for hb in range(4):
        pick = (((lane >> 2) & 3) == hb) & (low == 8 * (lane & 3) + (lane >> 4))
        part = jnp.dot(pixels[:, 8 * hb:8 * hb + 8, :].reshape(24, 32).astype(BF), jnp.where(pick, 1.0, 0.0).astype(BF),
                       preferred_element_type=F32)
        z = part if z is None else z + part
    spread_row, spread_lane = iota((24, 1024), 0), iota((24, 1024), 1)
    spread = ((spread_lane >> 7) == (spread_row & 7)) & ((spread_lane & 127) == (spread_row >> 3))
    z = jnp.dot(z.T.astype(BF), jnp.where(spread, 1.0, 0.0).astype(BF), preferred_element_type=F32).astype(BF)
    for hl in range(8):
        maps["x"][2 + hl, 2:10] = z[:, 128 * hl:128 * hl + 128].reshape(8, 16, 128)
    w27[...] = jnp.zeros(w27.shape, F32)
    for t in range(9):
        w27[pl.ds(3 * t, 3), :] = w_enc1a[t].astype(F32)

    pl.semaphore_wait(barrier, count)
    send("x")
    receive("x")

    def lanes_of(value, shift):
        return value if shift == 0 else pltpu.roll(value, shift, 1)

    for j in range(10):
        three = []
        for i in range(12):
            value = None
            for dx in range(3):
                part = lanes_of(maps["x"][i, j + dx].astype(F32), 3 * dx)
                value = part if value is None else value + part
            three.append(value)
        for i in range(10):
            nine = three[i] + lanes_of(three[i + 1], 9) + lanes_of(three[i + 2], 18)
            x27[i, j] = nine.astype(BF)

    @pl.when(go)
    def _():
        put("a1", act(jnp.dot(x27[...].reshape(1600, 128), w27[...].astype(BF), preferred_element_type=F32), "enc1a"), 1)

    clear_outside("a1")
    layer("s1", "a1", "enc1b", 192)
    pool("s1", "p1")
    send("p1")
    send("s1")
    receive("p1")
    layer("a2", "p1", "enc2a", 192, 1)
    clear_outside("a2")
    layer("s2", "a2", "enc2b", 384)
    pool("s2", "p2")
    send("p2")
    send("s2")
    receive("s1")
    w_copy["dec1a"].wait()

    @pl.when(go)
    def _():
        acc1[...] = conv_sum("s1", "dec1a", 192, 384)

    receive("p2")
    layer("ma", "p2", "mid_a", 384, 1)
    clear_outside("ma")
    w_copy["mid_b"].wait()

    @pl.when(go)
    def _():
        mb[...] = act(conv_sum("ma", "mid_b", 0, 768), "mid_b")

    up(mb, "up2", "u2")
    send("u2")
    receive("s2")
    w_copy["dec2a"].wait()

    @pl.when(go)
    def _():
        acc2[...] = conv_sum("s2", "dec2a", 384, 768)

    receive("u2")

    @pl.when(go)
    def _():
        put("e2", act(conv_sum("u2", "dec2a", 0, 768) + acc2[...], "dec2a"))

    send("e2")
    receive("e2")
    w_copy["dec2b"].wait()

    @pl.when(go)
    def _():
        d2[...] = act(conv_sum("e2", "dec2b", 0, 384), "dec2b")

    up(d2, "up1", "u1")
    send("u1")
    receive("u1")

    @pl.when(go)
    def _():
        put("e1", act(conv_sum("u1", "dec1a", 0, 384) + acc1[...], "dec1a"))

    send("e1")
    receive("e1")
    w_copy["dec1b"].wait()

    @pl.when(go)
    def _():
        d1[...] = act(conv_sum("e1", "dec1b", 0, 192), "dec1b")

    @pl.when(go)
    def _():
        out_channels = y_ref.shape[0]
        for hl in range(8):
            y_rows[:, hl, :] = rows_dot(w_head[...], d1[pl.ds(128 * hl, 128), :])
        k, n = iota((128, 128), 0), iota((128, 128), 1)
        pick = ((n >> 5) == ((k >> 2) & 3)) & ((n & 31) == 8 * (k & 3) + (k >> 4))
        y = jnp.dot(y_rows[...].reshape(8 * out_channels, 128), jnp.where(pick, 1.0, 0.0), precision=lax.Precision.HIGHEST,
                    preferred_element_type=F32).reshape(out_channels, 8, 128)
        for c in range(out_channels):
            for hb in range(4):
                y_ref[c, pl.ds(8 * hb, 8), :] = y[c, :, 32 * hb:32 * hb + 32] + b_head[c]

    for name in SHARED:
        for way in range(8):
            @pl.when(has[way])
            def _(way=way, name=name):
                copies(name, way).wait_send()


def solution(mesh):
    rows = mesh.shape["row"]
    cols = mesh.shape["col"]
    tile_spec = P(("data", "row"), "col", None)

    def device_body(image, *params):
        names = ("w_enc1a", "b_enc1a", "w_enc1b", "b_enc1b", "w_enc2a", "b_enc2a", "w_enc2b", "b_enc2b", "w_mid_a", "b_mid_a",
                 "w_mid_b", "b_mid_b", "w_up2", "w_dec2a", "b_dec2a", "w_dec2b", "b_dec2b", "w_up1", "w_dec1a", "b_dec1a",
                 "w_dec1b", "b_dec1b", "w_head", "b_head")
        p = dict(zip(names, params))
        high, wide, depth = image.shape
        weights = [p["w_" + n].swapaxes(2, 3) if n in TURNED else p["w_" + n] for n in WEIGHTS]
        weights = [w.reshape(-1, w.shape[-1]) for w in weights]
        biases = [p["b_" + n] for n in BIASES]
        vmem = pl.BlockSpec(memory_space=pltpu.VMEM)
        smem = pl.BlockSpec(memory_space=pltpu.SMEM)
        hbm = pl.BlockSpec(memory_space=pl.ANY)
        out_channels = p["w_head"].shape[1]
        scratch = [pltpu.VMEM(w.shape, BF) for w in weights]
        scratch += [pltpu.VMEM((s + 2 * r, s + 2 * r, 16, c), BF) for s, r, c in MAPS.values()]
        scratch += [pltpu.VMEM((4 * tiles_of(n) + 4, 16, MAPS[n][2]), BF) for n in SHARED] * 2
        scratch += [pltpu.VMEM((10, 10, 16, 128), BF), pltpu.VMEM((128, 192), F32), pltpu.VMEM((64, 768), BF),
                    pltpu.VMEM((256, 384), BF), pltpu.VMEM((1024, 192), BF), pltpu.VMEM((1024, 192), F32),
                    pltpu.VMEM((256, 384), F32), pltpu.VMEM((out_channels, 8, 128), F32)]
        scratch += [pltpu.SemaphoreType.DMA((len(WEIGHTS),)), pltpu.SemaphoreType.DMA((len(SHARED), 8)),
                    pltpu.SemaphoreType.DMA((len(SHARED), 8))]
        y = pl.pallas_call(
            functools.partial(body, rows, cols),
            out_shape=jax.ShapeDtypeStruct((out_channels, high, wide), F32),
            in_specs=[vmem] * 3 + [smem] + [hbm] * len(weights) + [vmem] * len(biases),
            out_specs=vmem,
            scratch_shapes=scratch,
            compiler_params=pltpu.CompilerParams(collective_id=0, has_side_effects=True, vmem_limit_bytes=62 * 1024 * 1024),
            name="unet",
        )(image.transpose(2, 0, 1), p["w_enc1a"].reshape(9, depth, -1), p["w_head"].T, p["b_head"], *weights, *biases)
        return y.transpose(1, 2, 0)

    def program(image, *params):
        mapped = jax.shard_map(device_body, mesh=mesh, in_specs=(tile_spec,) + tuple([P()] * len(params)), out_specs=tile_spec, check_vma=False)
        return mapped(image, *params)

    return program
```

time: 87.1 us -> 50.1 us (0.58)
  Pallas kernels: 67.6 us -> 48.4 us
  local copies, waits for them, and re-layouts: 19.1 us -> 1.54 us
    pallas_call x1, Pallas kernels: 67.6 us -> 48.4 us  [device_body(): pl.pallas_call(functools.partial(body, rows, cols), out_shape=jax.ShapeDt...]
    reshape x9 -> x0, local copies, waits for them, and re-layouts: 11 us -> none  [the longest x6 7.71 us: device_body(): biases = [p['b_' + n].reshape(1, -1) for n in BIASES]]
    unnamed x5 -> x1, local copies, waits for them, and re-layouts: 5.9 us -> 1.54 us
    transpose x1 -> x0, local copies, waits for them, and re-layouts: 2.17 us -> none  [device_body(): y.reshape(high // 4, wide // 4, 4, 4, out_channels).transpose(2, 0, 3, 1, 4)]
where the time goes in v1:
time: 50.1 us; the launch traced here: 49.9 us
  Pallas kernels  48.4 us (97%)
  local copies, waits for them, and re-layouts  1.54 us (3%)
    pallas_call x1, Pallas kernels, device_body(): pl.pallas_call(functools.partial(body, rows, cols), out_shape=jax.ShapeDt...  48.4 us
    unnamed x1, local copies, waits for them, and re-layouts  1.54 us

profile of v1, /device:TPU:97, one launch (start us, length us, event | category | flops | bytes accessed | tf_op | source)
XLA Modules:
  0.0 49.9 jit_solution(2115869533784910046)
XLA Ops:
  0.0 48.4 %unet.1 = f32[6,32,32]{2,1,0:T(8,128)} custom-call(bf16[3,32,32]{2,1,0:T(8,128)(2,1)} %bitcast.31, bf16[9,3,192]{2,1,0:T(4,128)(2,1)} %bitcast.32, bf16[6,192]{1,0:T(8,128)(2,1)} %bitcast.33, f32[6]{0:T(128)} %refs_3_.1, bf16[1728,192]{1,0:T(8,128)(2,1)} %bitcast.27, bf16[1728,384]{1,0:T(8,128)(2,1)} %bitcast.25, bf16[3456,384]{1,0:T(8,128)(2,1)} %bitcast.22, ...), custom_call_target="tpu_custom_call" | custom-call | tf_op jit(solution)/shard_map/unet/pallas_call | solution.py:410
  48.4 1.5 %copy.27 = f32[32,32,6]{1,0,2:T(8,128)} copy(f32[32,32,6]{1,0,2:T(8,128)} %bitcast.30) | data formatting | bytes 49152

commit v2 on v1

--- a/solution.py
+++ b/solution.py
@@ -15,9 +15,10 @@
 WEIGHTS = ("enc1b", "enc2a", "enc2b", "mid_a", "mid_b", "up2", "dec2a", "dec2b", "up1", "dec1a", "dec1b")
 TURNED = ("up1", "dec1a")
 BIASES = ("enc1a", "enc1b", "enc2a", "enc2b", "mid_a", "mid_b", "dec2a", "dec2b", "dec1a", "dec1b")
-MAPS = {"x": (8, 2, 128), "s1": (8, 1, 192), "p1": (4, 2, 192), "s2": (4, 1, 384), "p2": (2, 2, 384), "u2": (4, 1, 384),
-        "e2": (4, 1, 384), "u1": (8, 1, 192), "e1": (8, 1, 192), "a1": (8, 1, 192), "a2": (4, 1, 384), "ma": (2, 1, 768)}
-SHARED = ("x", "s1", "p1", "s2", "p2", "u2", "e2", "u1", "e1")
+MAPS = {"x": (8, 2, 128), "s1": (8, 2, 192), "p1": (4, 2, 192), "s2": (4, 2, 384), "p2": (2, 2, 384), "u2": (4, 2, 384),
+        "u1": (8, 2, 192), "a1": (8, 1, 192), "a2": (4, 1, 384), "ma": (2, 1, 768), "e2": (4, 1, 384), "e1": (8, 1, 192)}
+SHARED = ("x", "s1", "p1", "s2", "p2", "u2", "u1")
+SMALL = ("x", "w_enc1a", "w_head") + BIASES
 
 
 def tiles_of(name):
@@ -46,16 +47,20 @@
         del refs[:count]
         return head
 
-    x_ref, w_enc1a, w_head, b_head = take(4)
+    (b_head,) = take(1)
+    small_hbm = dict(zip(SMALL, take(len(SMALL))))
     w_hbm = dict(zip(WEIGHTS, take(len(WEIGHTS))))
-    bias = dict(zip(BIASES, take(len(BIASES))))
     (y_ref,) = take(1)
+    small = dict(zip(SMALL, take(len(SMALL))))
+    x_ref, w_enc1a, w_head, bias = small["x"], small["w_enc1a"], small["w_head"], small
     w_vm = dict(zip(WEIGHTS, take(len(WEIGHTS))))
     maps = dict(zip(MAPS, take(len(MAPS))))
     packs = dict(zip(SHARED, take(len(SHARED))))
     lands = dict(zip(SHARED, take(len(SHARED))))
+    corner_packs = dict(zip(SHARED, take(len(SHARED))))
+    corner_lands = dict(zip(SHARED, take(len(SHARED))))
     x27, w27, mb, d2, d1, acc1, acc2, y_rows = take(8)
-    w_sem, send_sem, recv_sem = take(3)
+    small_sem, w_sem, send_sem, recv_sem = take(4)
 
     data = lax.axis_index("data")
     row = lax.axis_index("row")
@@ -66,11 +71,6 @@
 
     def neighbour(way):
         return (data, col + STEP[way][1], row + STEP[way][0])
-
-    w_copy = {}
-    for index, name in enumerate(WEIGHTS):
-        w_copy[name] = pltpu.make_async_copy(w_hbm[name], w_vm[name], w_sem.at[index])
-        w_copy[name].start()
 
     barrier = pltpu.get_barrier_semaphore()
     count = jnp.int32(0)
@@ -80,13 +80,19 @@
             pl.semaphore_signal(barrier, inc=1, device_id=neighbour(way), device_id_type=MESH)
         count = count + has[way].astype(jnp.int32)
 
+    small_copy = {}
+    for index, name in enumerate(SMALL):
+        small_copy[name] = pltpu.make_async_copy(small_hbm[name], small[name], small_sem.at[index])
+        small_copy[name].start()
+    w_copy = {}
+    for index, name in enumerate(WEIGHTS):
+        w_copy[name] = pltpu.make_async_copy(w_hbm[name], w_vm[name], w_sem.at[index])
+
     def land(name, way):
-        tiles = tiles_of(name)
-        return lands[name].at[pl.ds(way * tiles, tiles)] if way < 4 else lands[name].at[pl.ds(4 * tiles + way - 4, 1)]
+        return lands[name].at[way] if way < 4 else corner_lands[name].at[way - 4]
 
     def pack(name, way):
-        tiles = tiles_of(name)
-        return packs[name].at[pl.ds(way * tiles, tiles)] if way < 4 else packs[name].at[pl.ds(4 * tiles + way - 4, 1)]
+        return packs[name].at[way] if way < 4 else corner_packs[name].at[way - 4]
 
     def copies(name, way):
         index = SHARED.index(name)
@@ -136,7 +142,10 @@
                         test = s == k
                     packed[t] = value if t not in packed else jnp.where(test, value, packed[t])
             for t, value in packed.items():
-                packs[name][(way * tiles if way < 4 else 4 * tiles + way - 4) + t] = value.astype(BF)
+                if way < 4:
+                    packs[name][way, t] = value.astype(BF)
+                else:
+                    corner_packs[name][way - 4] = value[0:8].astype(BF)
         for way in range(8):
             @pl.when(has[way])
             def _(way=way):
@@ -153,7 +162,10 @@
         zero = jnp.zeros((16, channels), F32)
 
         def came(way, tile):
-            value = lands[name][(way * tiles if way < 4 else 4 * tiles + way - 4) + tile].astype(F32)
+            if way < 4:
+                value = lands[name][way, tile].astype(F32)
+            else:
+                value = jnp.concatenate([corner_lands[name][way - 4].astype(F32), zero[0:8]], axis=0)
             return jnp.where(has[way], value, zero)
 
         for i in range(-ring, side + ring):
@@ -255,6 +267,10 @@
                             maps[target][ring + 2 * i + p, ring + 2 * j + q] = out[i, j]
 
     lane, low = iota((32, 128), 1), iota((32, 128), 0)
+    for name in SMALL:
+        small_copy[name].wait()
+    for name in WEIGHTS:
+        w_copy[name].start()
     pixels = x_ref[...].astype(F32)
     z = None
     for hb in range(4):
@@ -298,22 +314,22 @@
     layer("s1", "a1", "enc1b", 192)
     pool("s1", "p1")
     send("p1")
+    receive("p1")
     send("s1")
-    receive("p1")
     layer("a2", "p1", "enc2a", 192, 1)
     clear_outside("a2")
     layer("s2", "a2", "enc2b", 384)
     pool("s2", "p2")
     send("p2")
-    send("s2")
     receive("s1")
     w_copy["dec1a"].wait()
 
     @pl.when(go)
     def _():
-        acc1[...] = conv_sum("s1", "dec1a", 192, 384)
+        acc1[...] = conv_sum("s1", "dec1a", 192, 384, 1)
 
     receive("p2")
+    send("s2")
     layer("ma", "p2", "mid_a", 384, 1)
     clear_outside("ma")
     w_copy["mid_b"].wait()
@@ -329,16 +345,15 @@
 
     @pl.when(go)
     def _():
-        acc2[...] = conv_sum("s2", "dec2a", 384, 768)
+        acc2[...] = conv_sum("s2", "dec2a", 384, 768, 1)
 
     receive("u2")
 
     @pl.when(go)
     def _():
-        put("e2", act(conv_sum("u2", "dec2a", 0, 768) + acc2[...], "dec2a"))
-
-    send("e2")
-    receive("e2")
+        put("e2", act(conv_sum("u2", "dec2a", 0, 768, 1) + acc2[...], "dec2a"), 1)
+
+    clear_outside("e2")
     w_copy["dec2b"].wait()
 
     @pl.when(go)
@@ -351,10 +366,9 @@
 
     @pl.when(go)
     def _():
-        put("e1", act(conv_sum("u1", "dec1a", 0, 384) + acc1[...], "dec1a"))
-
-    send("e1")
-    receive("e1")
+        put("e1", act(conv_sum("u1", "dec1a", 0, 384, 1) + acc1[...], "dec1a"), 1)
+
+    clear_outside("e1")
     w_copy["dec1b"].wait()
 
     @pl.when(go)
@@ -399,23 +413,25 @@
         smem = pl.BlockSpec(memory_space=pltpu.SMEM)
         hbm = pl.BlockSpec(memory_space=pl.ANY)
         out_channels = p["w_head"].shape[1]
-        scratch = [pltpu.VMEM(w.shape, BF) for w in weights]
+        smalls = [image.transpose(2, 0, 1), p["w_enc1a"].reshape(9, depth, -1), p["w_head"].T] + biases
+        scratch = [pltpu.VMEM(a.shape, a.dtype) for a in smalls + weights]
         scratch += [pltpu.VMEM((s + 2 * r, s + 2 * r, 16, c), BF) for s, r, c in MAPS.values()]
-        scratch += [pltpu.VMEM((4 * tiles_of(n) + 4, 16, MAPS[n][2]), BF) for n in SHARED] * 2
+        scratch += [pltpu.VMEM((4, tiles_of(n), 16, MAPS[n][2]), BF) for n in SHARED] * 2
+        scratch += [pltpu.VMEM((4, 8, MAPS[n][2]), BF) for n in SHARED] * 2
         scratch += [pltpu.VMEM((10, 10, 16, 128), BF), pltpu.VMEM((128, 192), F32), pltpu.VMEM((64, 768), BF),
-                    pltpu.VMEM((256, 384), BF), pltpu.VMEM((1024, 192), BF), pltpu.VMEM((1024, 192), F32),
-                    pltpu.VMEM((256, 384), F32), pltpu.VMEM((out_channels, 8, 128), F32)]
-        scratch += [pltpu.SemaphoreType.DMA((len(WEIGHTS),)), pltpu.SemaphoreType.DMA((len(SHARED), 8)),
+                    pltpu.VMEM((256, 384), BF), pltpu.VMEM((1024, 192), BF), pltpu.VMEM((1600, 192), F32),
+                    pltpu.VMEM((576, 384), F32), pltpu.VMEM((out_channels, 8, 128), F32)]
+        scratch += [pltpu.SemaphoreType.DMA((len(SMALL),)), pltpu.SemaphoreType.DMA((len(WEIGHTS),)), pltpu.SemaphoreType.DMA((len(SHARED), 8)),
                     pltpu.SemaphoreType.DMA((len(SHARED), 8))]
         y = pl.pallas_call(
             functools.partial(body, rows, cols),
             out_shape=jax.ShapeDtypeStruct((out_channels, high, wide), F32),
-            in_specs=[vmem] * 3 + [smem] + [hbm] * len(weights) + [vmem] * len(biases),
+            in_specs=[smem] + [hbm] * (len(smalls) + len(weights)),
             out_specs=vmem,
             scratch_shapes=scratch,
             compiler_params=pltpu.CompilerParams(collective_id=0, has_side_effects=True, vmem_limit_bytes=62 * 1024 * 1024),
             name="unet",
-        )(image.transpose(2, 0, 1), p["w_enc1a"].reshape(9, depth, -1), p["w_head"].T, p["b_head"], *weights, *biases)
+        )(p["b_head"], *smalls, *weights)
         return y.transpose(1, 2, 0)
 
     def program(image, *params):

time: 50.1 us -> 47.3 us (0.944)
  Pallas kernels: 48.4 us -> 45.5 us
    pallas_call x1, Pallas kernels: 48.4 us -> 45.5 us  [device_body(): pl.pallas_call(functools.partial(body, rows, cols), out_shape=jax.ShapeDt...]
where the time goes in v2:
time: 47.3 us; the launch traced here: 47.1 us
  Pallas kernels  45.5 us (96%)
  local copies, waits for them, and re-layouts  1.54 us (3%)
    pallas_call x1, Pallas kernels, device_body(): pl.pallas_call(functools.partial(body, rows, cols), out_shape=jax.ShapeDt...  45.5 us
    unnamed x1, local copies, waits for them, and re-layouts  1.54 us

profile of v2, /device:TPU:97, one launch (start us, length us, event | category | flops | bytes accessed | tf_op | source)
XLA Modules:
  0.0 47.1 jit_solution(6460422840430731302)
XLA Ops:
  0.0 45.5 %unet.1 = f32[6,32,32]{2,1,0:T(8,128)} custom-call(f32[6]{0:T(128)} %refs_0_.1, bf16[3,32,32]{2,1,0:T(8,128)(2,1)} %bitcast.31, bf16[9,3,192]{2,1,0:T(4,128)(2,1)} %bitcast.32, bf16[6,192]{1,0:T(8,128)(2,1)} %bitcast.33, f32[192]{0:T(256)} %refs_4_.1, f32[192]{0:T(256)} %refs_5_.1, f32[384]{0:T(512)} %refs_6_.1, f32[384]{0:T(512)} %refs_7_.1, f32[768]{0:T(1024)} %refs_8_.1, ...), custom_call_target="tpu_custom_call" | custom-call | tf_op jit(solution)/shard_map/unet/pallas_call | solution.py:426
  45.5 1.5 %copy.27 = f32[32,32,6]{1,0,2:T(8,128)} copy(f32[32,32,6]{1,0,2:T(8,128)} %bitcast.30) | data formatting | bytes 49152

commit v3 on v2

--- a/solution.py
+++ b/solution.py
@@ -214,16 +214,61 @@
         return [m[first + dy:first + dy + size, first + dx:first + dx + size].reshape(size * size * 16, channels)
                 for dy in range(3) for dx in range(3)]
 
+    def tap_weight(weight, t, count, first, channels, depth):
+        if depth == channels:
+            return w_vm[weight][pl.ds(t * depth, count * depth), :]
+        parts = [w_vm[weight][pl.ds(u * depth + first, channels), :] for u in range(t, t + count)]
+        return parts[0] if count == 1 else jnp.concatenate(parts, axis=0)
+
+    def chain(values, numbers, weight, first, channels, depth):
+        total, at = None, 0
+        while at < len(values):
+            count = 1
+            if channels == 384 and weight not in TURNED:
+                while count < 2 and at + count < len(values) and numbers[at + count] == numbers[at] + count:
+                    count += 1
+            value = values[at] if count == 1 else jnp.concatenate(values[at:at + count], axis=1)
+            if weight in TURNED:
+                part = rows_dot(value, w_vm[weight][pl.ds(numbers[at] * 192, 192), first:first + channels])
+            else:
+                part = jnp.dot(value, tap_weight(weight, numbers[at], count, first, channels, depth), preferred_element_type=F32)
+            total = part if total is None else total + part
+            at += count
+        return total
+
     def conv_sum(name, weight, first, depth, out_ring=0):
-        total = None
-        channels = MAPS[name][2]
-        for t, tap in enumerate(taps(name, out_ring)):
-            if weight in TURNED:
-                part = rows_dot(tap, w_vm[weight][pl.ds(t * 192, 192), first:first + channels])
-            else:
-                part = jnp.dot(tap, w_vm[weight][pl.ds(t * depth + first, channels), :], preferred_element_type=F32)
-            total = part if total is None else total + part
-        return total
+        return chain(taps(name, out_ring), range(9), weight, first, MAPS[name][2], depth)
+
+    def clear_ring(name):
+        side, ring, channels = MAPS[name]
+        m, wide = maps[name], side + 2 * ring
+        flat, tall = jnp.zeros((ring, wide, 16, channels), BF), jnp.zeros((side, ring, 16, channels), BF)
+        m[0:ring] = flat
+        m[side + ring:wide] = flat
+        m[ring:side + ring, 0:ring] = tall
+        m[ring:side + ring, side + ring:wide] = tall
+
+    def ring_sum(name, weight, first, depth, acc):
+        side, ring, channels = MAPS[name]
+        m, size = maps[name], side + 2
+        lines = ((0, 1), (0, size - 1), (size - 2, size - 1))
+        blank = jnp.zeros((2, 16, channels), BF)
+
+        def product(values, numbers):
+            values = [v.reshape(2 * size * 16, channels) for v in values]
+            return chain(values, numbers, weight, first, channels, depth).reshape(2, size, 16, -1)
+
+        for dy in range(3):
+            out = product([jnp.concatenate([m[r + dy, dx:dx + size] for r in lines[dy]], axis=0) for dx in range(3)],
+                          [3 * dy + dx for dx in range(3)])
+            for n, r in enumerate(lines[dy]):
+                acc[r] = acc[r] + out[n]
+        for dx in range(3):
+            strips = [jnp.concatenate([blank, m[2:side + 2, r + dx], blank], axis=0) for r in lines[dx]]
+            out = product([jnp.concatenate([strip[dy:dy + size] for strip in strips], axis=0) for dy in range(3)],
+                          [3 * dy + dx for dy in range(3)])
+            for n, r in enumerate(lines[dx]):
+                acc[:, r] = acc[:, r] + out[n]
 
     def act(total, name):
         return jnp.maximum(total + bias[name][...][None, :], 0.0).astype(BF)
@@ -289,6 +334,8 @@
 
     pl.semaphore_wait(barrier, count)
     send("x")
+    clear_ring("u1")
+    clear_ring("p1")
     receive("x")
 
     def lanes_of(value, shift):
@@ -314,9 +361,23 @@
     layer("s1", "a1", "enc1b", 192)
     pool("s1", "p1")
     send("p1")
+    w_copy["enc2a"].wait()
+
+    @pl.when(go)
+    def _():
+        acc2[...] = conv_sum("p1", "enc2a", 0, 192, 1).reshape(acc2.shape)
+
     receive("p1")
     send("s1")
-    layer("a2", "p1", "enc2a", 192, 1)
+
+    @pl.when(go)
+    def _():
+        ring_sum("p1", "enc2a", 0, 192, acc2)
+
+    @pl.when(go)
+    def _():
+        put("a2", act(acc2[...].reshape(576, 384), "enc2a"), 1)
+
     clear_outside("a2")
     layer("s2", "a2", "enc2b", 384)
     pool("s2", "p2")
@@ -326,7 +387,7 @@
 
     @pl.when(go)
     def _():
-        acc1[...] = conv_sum("s1", "dec1a", 192, 384, 1)
+        acc1[...] = conv_sum("s1", "dec1a", 192, 384, 1).reshape(acc1.shape)
 
     receive("p2")
     send("s2")
@@ -345,13 +406,13 @@
 
     @pl.when(go)
     def _():
-        acc2[...] = conv_sum("s2", "dec2a", 384, 768, 1)
+        acc2[...] = conv_sum("s2", "dec2a", 384, 768, 1).reshape(acc2.shape)
 
     receive("u2")
 
     @pl.when(go)
     def _():
-        put("e2", act(conv_sum("u2", "dec2a", 0, 768, 1) + acc2[...], "dec2a"), 1)
+        put("e2", act(conv_sum("u2", "dec2a", 0, 768, 1) + acc2[...].reshape(576, 384), "dec2a"), 1)
 
     clear_outside("e2")
     w_copy["dec2b"].wait()
@@ -362,11 +423,20 @@
 
     up(d2, "up1", "u1")
     send("u1")
+
+    @pl.when(go)
+    def _():
+        acc1[...] = acc1[...] + conv_sum("u1", "dec1a", 0, 384, 1).reshape(acc1.shape)
+
     receive("u1")
 
     @pl.when(go)
     def _():
-        put("e1", act(conv_sum("u1", "dec1a", 0, 384, 1) + acc1[...], "dec1a"), 1)
+        ring_sum("u1", "dec1a", 0, 384, acc1)
+
+    @pl.when(go)
+    def _():
+        put("e1", act(acc1[...].reshape(1600, 192), "dec1a"), 1)
 
     clear_outside("e1")
     w_copy["dec1b"].wait()
@@ -419,8 +489,8 @@
         scratch += [pltpu.VMEM((4, tiles_of(n), 16, MAPS[n][2]), BF) for n in SHARED] * 2
         scratch += [pltpu.VMEM((4, 8, MAPS[n][2]), BF) for n in SHARED] * 2
         scratch += [pltpu.VMEM((10, 10, 16, 128), BF), pltpu.VMEM((128, 192), F32), pltpu.VMEM((64, 768), BF),
-                    pltpu.VMEM((256, 384), BF), pltpu.VMEM((1024, 192), BF), pltpu.VMEM((1600, 192), F32),
-                    pltpu.VMEM((576, 384), F32), pltpu.VMEM((out_channels, 8, 128), F32)]
+                    pltpu.VMEM((256, 384), BF), pltpu.VMEM((1024, 192), BF), pltpu.VMEM((10, 10, 16, 192), F32),
+                    pltpu.VMEM((6, 6, 16, 384), F32), pltpu.VMEM((out_channels, 8, 128), F32)]
         scratch += [pltpu.SemaphoreType.DMA((len(SMALL),)), pltpu.SemaphoreType.DMA((len(WEIGHTS),)), pltpu.SemaphoreType.DMA((len(SHARED), 8)),
                     pltpu.SemaphoreType.DMA((len(SHARED), 8))]
         y = pl.pallas_call(

time: 47.3 us -> 44.8 us (0.947)
  Pallas kernels: 45.5 us -> 43.1 us
    pallas_call x1, Pallas kernels: 45.5 us -> 43.1 us  [device_body(): pl.pallas_call(functools.partial(body, rows, cols), out_shape=jax.ShapeDt...]
where the time goes in v3:
time: 44.8 us; the launch traced here: 44.6 us
  Pallas kernels  43.1 us (96%)
  local copies, waits for them, and re-layouts  1.54 us (3%)
    pallas_call x1, Pallas kernels, device_body(): pl.pallas_call(functools.partial(body, rows, cols), out_shape=jax.ShapeDt...  43.1 us
    unnamed x1, local copies, waits for them, and re-layouts  1.54 us

profile of v3, /device:TPU:97, one launch (start us, length us, event | category | flops | bytes accessed | tf_op | source)
XLA Modules:
  0.0 44.6 jit_solution(14257648648888036992)
XLA Ops:
  0.0 43.1 %unet.1 = f32[6,32,32]{2,1,0:T(8,128)} custom-call(f32[6]{0:T(128)} %refs_0_.1, bf16[3,32,32]{2,1,0:T(8,128)(2,1)} %bitcast.31, bf16[9,3,192]{2,1,0:T(4,128)(2,1)} %bitcast.32, bf16[6,192]{1,0:T(8,128)(2,1)} %bitcast.33, f32[192]{0:T(256)} %refs_4_.1, f32[192]{0:T(256)} %refs_5_.1, f32[384]{0:T(512)} %refs_6_.1, f32[384]{0:T(512)} %refs_7_.1, f32[768]{0:T(1024)} %refs_8_.1, ...), custom_call_target="tpu_custom_call" | custom-call | tf_op jit(solution)/shard_map/unet/pallas_call | solution.py:496
  43.1 1.5 %copy.27 = f32[32,32,6]{1,0,2:T(8,128)} copy(f32[32,32,6]{1,0,2:T(8,128)} %bitcast.30) | data formatting | bytes 49152

commit v4 on v3

--- a/solution.py
+++ b/solution.py
@@ -12,6 +12,7 @@
 F32 = jnp.float32
 STEP = ((-1, 0), (1, 0), (0, -1), (0, 1), (-1, -1), (-1, 1), (1, -1), (1, 1))
 OPPOSITE = (1, 0, 3, 2, 7, 6, 5, 4)
+ORDER = (2, 3, 4, 5, 6, 7, 0, 1)
 WEIGHTS = ("enc1b", "enc2a", "enc2b", "mid_a", "mid_b", "up2", "dec2a", "dec2b", "up1", "dec1a", "dec1b")
 TURNED = ("up1", "dec1a")
 BIASES = ("enc1a", "enc1b", "enc2a", "enc2b", "mid_a", "mid_b", "dec2a", "dec2b", "dec1a", "dec1b")
@@ -120,7 +121,7 @@
     def span(side, ring, d):
         return range(side) if d == 0 else range(ring) if d < 0 else range(side - ring, side)
 
-    def send(name):
+    def gather(name):
         side, ring, channels = MAPS[name]
         m, tiles = maps[name], tiles_of(name)
         s = sublane(channels)
@@ -130,7 +131,7 @@
             for i in span(side, ring, di):
                 for j in span(side, ring, dj):
                     e = spot(name, way, i, j)
-                    value = m[ring + i, ring + j].astype(F32)
+                    value = m[ring + i, ring + j]
                     edge = 4 * (3 if di > 0 else 0) + (3 if dj > 0 else 0)
                     if way < 4:
                         t, k = e // 4, e % 4
@@ -143,13 +144,26 @@
                     packed[t] = value if t not in packed else jnp.where(test, value, packed[t])
             for t, value in packed.items():
                 if way < 4:
-                    packs[name][way, t] = value.astype(BF)
+                    packs[name][way, t] = value
                 else:
-                    corner_packs[name][way - 4] = value[0:8].astype(BF)
-        for way in range(8):
+                    corner_packs[name][way - 4] = value[0:8]
+
+    def launch(name):
+        for way in ORDER:
             @pl.when(has[way])
             def _(way=way):
                 copies(name, way).start()
+
+    def settle(names):
+        for name in names:
+            for way in range(8):
+                @pl.when(has[way])
+                def _(way=way, name=name):
+                    copies(name, way).wait_send()
+
+    def send(name):
+        gather(name)
+        launch(name)
 
     def receive(name):
         for way in range(8):
@@ -159,13 +173,13 @@
         side, ring, channels = MAPS[name]
         m, tiles = maps[name], tiles_of(name)
         s = sublane(channels)
-        zero = jnp.zeros((16, channels), F32)
+        zero = jnp.zeros((16, channels), BF)
 
         def came(way, tile):
             if way < 4:
-                value = lands[name][way, tile].astype(F32)
+                value = lands[name][way, tile]
             else:
-                value = jnp.concatenate([corner_lands[name][way - 4].astype(F32), zero[0:8]], axis=0)
+                value = jnp.concatenate([corner_lands[name][way - 4], zero[0:8]], axis=0)
             return jnp.where(has[way], value, zero)
 
         for i in range(-ring, side + ring):
@@ -175,7 +189,7 @@
                 if di == 0 and dj == 0:
                     continue
                 si, sj = i % side, j % side
-                value = turn(m[ring + si, ring + sj].astype(F32), -4 * di - dj)
+                value = turn(m[ring + si, ring + sj], -4 * di - dj)
                 hb, wb = (3 if di > 0 else 0), (3 if dj > 0 else 0)
                 if di:
                     way = STEP.index((di, 0))
@@ -189,13 +203,13 @@
                     way = STEP.index((di, dj))
                     e = spot(name, OPPOSITE[way], si, sj)
                     value = jnp.where(s == 4 * hb + wb, turn(came(way, 0), 4 * hb + wb - e), value)
-                m[ring + i, ring + j] = value.astype(BF)
+                m[ring + i, ring + j] = value
 
     def clear_outside(name):
         side, ring, channels = MAPS[name]
         m = maps[name]
         s = sublane(channels)
-        zero = jnp.zeros((16, channels), F32)
+        zero = jnp.zeros((16, channels), BF)
         inside = [None] * 4
         for way, test in enumerate(((s >> 2) == 0, (s >> 2) == 3, (s & 3) == 0, (s & 3) == 3)):
             inside[way] = jnp.logical_or(jnp.logical_not(test), has[way])
@@ -203,10 +217,10 @@
             for j in range(-ring, side + ring):
                 ways = [w for w, out in enumerate((i < 0, i >= side, j < 0, j >= side)) if out]
                 if ways:
-                    value = m[ring + i, ring + j].astype(F32)
+                    value = m[ring + i, ring + j]
                     for way in ways:
                         value = jnp.where(inside[way], value, zero)
-                    m[ring + i, ring + j] = value.astype(BF)
+                    m[ring + i, ring + j] = value
 
     def taps(name, out_ring):
         side, ring, channels = MAPS[name]
@@ -346,12 +360,12 @@
         for i in range(12):
             value = None
             for dx in range(3):
-                part = lanes_of(maps["x"][i, j + dx].astype(F32), 3 * dx)
+                part = lanes_of(maps["x"][i, j + dx], 3 * dx)
                 value = part if value is None else value + part
             three.append(value)
         for i in range(10):
             nine = three[i] + lanes_of(three[i + 1], 9) + lanes_of(three[i + 2], 18)
-            x27[i, j] = nine.astype(BF)
+            x27[i, j] = nine
 
     @pl.when(go)
     def _():
@@ -367,8 +381,9 @@
     def _():
         acc2[...] = conv_sum("p1", "enc2a", 0, 192, 1).reshape(acc2.shape)
 
+    gather("s1")
     receive("p1")
-    send("s1")
+    launch("s1")
 
     @pl.when(go)
     def _():
@@ -382,6 +397,7 @@
     layer("s2", "a2", "enc2b", 384)
     pool("s2", "p2")
     send("p2")
+    gather("s2")
     receive("s1")
     w_copy["dec1a"].wait()
 
@@ -390,7 +406,7 @@
         acc1[...] = conv_sum("s1", "dec1a", 192, 384, 1).reshape(acc1.shape)
 
     receive("p2")
-    send("s2")
+    launch("s2")
     layer("ma", "p2", "mid_a", 384, 1)
     clear_outside("ma")
     w_copy["mid_b"].wait()
@@ -428,6 +444,7 @@
     def _():
         acc1[...] = acc1[...] + conv_sum("u1", "dec1a", 0, 384, 1).reshape(acc1.shape)
 
+    settle(SHARED[:-1])
     receive("u1")
 
     @pl.when(go)
@@ -458,11 +475,7 @@
             for hb in range(4):
                 y_ref[c, pl.ds(8 * hb, 8), :] = y[c, :, 32 * hb:32 * hb + 32] + b_head[c]
 
-    for name in SHARED:
-        for way in range(8):
-            @pl.when(has[way])
-            def _(way=way, name=name):
-                copies(name, way).wait_send()
+    settle(SHARED[-1:])
 
 
 def solution(mesh):

time: 44.8 us -> 42.2 us (0.942)
  Pallas kernels: 43.1 us -> 40.5 us
    pallas_call x1, Pallas kernels: 43.1 us -> 40.5 us  [device_body(): pl.pallas_call(functools.partial(body, rows, cols), out_shape=jax.ShapeDt...]
where the time goes in v4:
time: 42.2 us; the launch traced here: 42 us
  Pallas kernels  40.5 us (96%)
  local copies, waits for them, and re-layouts  1.54 us (4%)
    pallas_call x1, Pallas kernels, device_body(): pl.pallas_call(functools.partial(body, rows, cols), out_shape=jax.ShapeDt...  40.5 us
    unnamed x1, local copies, waits for them, and re-layouts  1.54 us

profile of v4, /device:TPU:97, one launch (start us, length us, event | category | flops | bytes accessed | tf_op | source)
XLA Modules:
  0.0 42.0 jit_solution(1527876443984020776)
XLA Ops:
  0.0 40.5 %unet.1 = f32[6,32,32]{2,1,0:T(8,128)} custom-call(f32[6]{0:T(128)} %refs_0_.1, bf16[3,32,32]{2,1,0:T(8,128)(2,1)} %bitcast.31, bf16[9,3,192]{2,1,0:T(4,128)(2,1)} %bitcast.32, bf16[6,192]{1,0:T(8,128)(2,1)} %bitcast.33, f32[192]{0:T(256)} %refs_4_.1, f32[192]{0:T(256)} %refs_5_.1, f32[384]{0:T(512)} %refs_6_.1, f32[384]{0:T(512)} %refs_7_.1, f32[768]{0:T(1024)} %refs_8_.1, ...), custom_call_target="tpu_custom_call" | custom-call | tf_op jit(solution)/shard_map/unet/pallas_call | solution.py:509
  40.5 1.5 %copy.27 = f32[32,32,6]{1,0,2:T(8,128)} copy(f32[32,32,6]{1,0,2:T(8,128)} %bitcast.30) | data formatting | bytes 49152

commit v5 on v4

--- a/solution.py
+++ b/solution.py
@@ -60,7 +60,7 @@
     lands = dict(zip(SHARED, take(len(SHARED))))
     corner_packs = dict(zip(SHARED, take(len(SHARED))))
     corner_lands = dict(zip(SHARED, take(len(SHARED))))
-    x27, w27, mb, d2, d1, acc1, acc2, y_rows = take(8)
+    x27, w27, mb, d2, d1, acc1, acc2, acc3, y_rows = take(9)
     small_sem, w_sem, send_sem, recv_sem = take(4)
 
     data = lax.axis_index("data")
@@ -250,8 +250,9 @@
             at += count
         return total
 
-    def conv_sum(name, weight, first, depth, out_ring=0):
-        return chain(taps(name, out_ring), range(9), weight, first, MAPS[name][2], depth)
+    def conv_sum(name, weight, first, depth, out_ring=0, some=range(9)):
+        values = taps(name, out_ring)
+        return chain([values[t] for t in some], some, weight, first, MAPS[name][2], depth)
 
     def clear_ring(name):
         side, ring, channels = MAPS[name]
@@ -262,8 +263,9 @@
         m[ring:side + ring, 0:ring] = tall
         m[ring:side + ring, side + ring:wide] = tall
 
-    def ring_sum(name, weight, first, depth, acc):
-        side, ring, channels = MAPS[name]
+    def ring_sum(name, weight, first, depth, acc, side=None):
+        channels = MAPS[name][2]
+        side = MAPS[name][0] if side is None else side
         m, size = maps[name], side + 2
         lines = ((0, 1), (0, size - 1), (size - 2, size - 1))
         blank = jnp.zeros((2, 16, channels), BF)
@@ -292,12 +294,13 @@
         size, first = side + 2 * out_ring, ring - out_ring
         maps[name][first:first + size, first:first + size] = value.reshape(size, size, 16, channels)
 
-    def layer(target, source, weight, depth, out_ring=0):
+    def layer(target, source, weight, depth, out_ring=0, after=None):
         w_copy[weight].wait()
 
         @pl.when(go)
         def _():
             put(target, act(conv_sum(source, weight, 0, depth, out_ring), weight), out_ring)
+            after()
 
     def pool(source, target):
         side, ring, channels = MAPS[target]
@@ -324,6 +327,7 @@
                     for i in range(side // 2):
                         for j in range(side // 2):
                             maps[target][ring + 2 * i + p, ring + 2 * j + q] = out[i, j]
+            gather(target)
 
     lane, low = iota((32, 128), 1), iota((32, 128), 0)
     for name in SMALL:
@@ -347,34 +351,66 @@
         w27[pl.ds(3 * t, 3), :] = w_enc1a[t].astype(F32)
 
     pl.semaphore_wait(barrier, count)
+    def lanes_of(value, shift):
+        return value if shift == 0 else pltpu.roll(value, shift, 1)
+
+    def patches(columns, lines):
+        for j in columns:
+            three = {}
+            for i in sorted({i + d for i in lines for d in range(3)}):
+                value = None
+                for dx in range(3):
+                    part = lanes_of(maps["x"][i, j + dx], 3 * dx)
+                    value = part if value is None else value + part
+                three[i] = value
+            for i in lines:
+                x27[i, j] = three[i] + lanes_of(three[i + 1], 9) + lanes_of(three[i + 2], 18)
+
+    def enc1a(value):
+        return act(jnp.dot(value.reshape(-1, 128), w27[...].astype(BF), preferred_element_type=F32), "enc1a").reshape(-1, 16, 192)
+
     send("x")
+    patches(range(2, 8), range(2, 8))
     clear_ring("u1")
     clear_ring("p1")
+    a1 = maps["a1"]
+    a1[0:2] = jnp.zeros((2, 10, 16, 192), BF)
+    a1[8:10] = jnp.zeros((2, 10, 16, 192), BF)
+    a1[2:8, 0:2] = jnp.zeros((6, 2, 16, 192), BF)
+    a1[2:8, 8:10] = jnp.zeros((6, 2, 16, 192), BF)
+
+    @pl.when(go)
+    def _():
+        a1[2:8, 2:8] = enc1a(x27[2:8, 2:8]).reshape(6, 6, 16, 192)
+
+    w_copy["enc1b"].wait()
+
+    @pl.when(go)
+    def _():
+        acc3[...] = conv_sum("a1", "enc1b", 0, 192).reshape(acc3.shape)
+
     receive("x")
-
-    def lanes_of(value, shift):
-        return value if shift == 0 else pltpu.roll(value, shift, 1)
-
-    for j in range(10):
-        three = []
-        for i in range(12):
-            value = None
-            for dx in range(3):
-                part = lanes_of(maps["x"][i, j + dx], 3 * dx)
-                value = part if value is None else value + part
-            three.append(value)
-        for i in range(10):
-            nine = three[i] + lanes_of(three[i + 1], 9) + lanes_of(three[i + 2], 18)
-            x27[i, j] = nine
-
-    @pl.when(go)
-    def _():
-        put("a1", act(jnp.dot(x27[...].reshape(1600, 128), w27[...].astype(BF), preferred_element_type=F32), "enc1a"), 1)
-
-    clear_outside("a1")
-    layer("s1", "a1", "enc1b", 192)
-    pool("s1", "p1")
-    send("p1")
+    patches(range(2, 8), (0, 1, 8, 9))
+    patches((0, 1, 8, 9), range(10))
+
+    @pl.when(go)
+    def _():
+        out = enc1a(jnp.concatenate([x27[0:2].reshape(20, 16, 128), x27[8:10].reshape(20, 16, 128),
+                                     x27[2:8, 0:2].reshape(12, 16, 128), x27[2:8, 8:10].reshape(12, 16, 128)], axis=0))
+        a1[0:2] = out[0:20].reshape(2, 10, 16, 192)
+        a1[8:10] = out[20:40].reshape(2, 10, 16, 192)
+        a1[2:8, 0:2] = out[40:52].reshape(6, 2, 16, 192)
+        a1[2:8, 8:10] = out[52:64].reshape(6, 2, 16, 192)
+        clear_outside("a1")
+
+    @pl.when(go)
+    def _():
+        ring_sum("a1", "enc1b", 0, 192, acc3, 6)
+        put("s1", act(acc3[...].reshape(1024, 192), "enc1b"))
+        pool("s1", "p1")
+        gather("p1")
+
+    launch("p1")
     w_copy["enc2a"].wait()
 
     @pl.when(go)
@@ -388,27 +424,27 @@
     @pl.when(go)
     def _():
         ring_sum("p1", "enc2a", 0, 192, acc2)
-
-    @pl.when(go)
-    def _():
         put("a2", act(acc2[...].reshape(576, 384), "enc2a"), 1)
-
-    clear_outside("a2")
-    layer("s2", "a2", "enc2b", 384)
-    pool("s2", "p2")
-    send("p2")
+        clear_outside("a2")
+
+
+    def halve():
+        pool("s2", "p2")
+        gather("p2")
+
+    layer("s2", "a2", "enc2b", 384, 0, halve)
+    launch("p2")
     gather("s2")
     receive("s1")
     w_copy["dec1a"].wait()
 
     @pl.when(go)
     def _():
-        acc1[...] = conv_sum("s1", "dec1a", 192, 384, 1).reshape(acc1.shape)
+        acc1[...] = conv_sum("s1", "dec1a", 192, 384, 1, range(6)).reshape(acc1.shape)
 
     receive("p2")
     launch("s2")
-    layer("ma", "p2", "mid_a", 384, 1)
-    clear_outside("ma")
+    layer("ma", "p2", "mid_a", 384, 1, lambda: clear_outside("ma"))
     w_copy["mid_b"].wait()
 
     @pl.when(go)
@@ -416,7 +452,7 @@
         mb[...] = act(conv_sum("ma", "mid_b", 0, 768), "mid_b")
 
     up(mb, "up2", "u2")
-    send("u2")
+    launch("u2")
     receive("s2")
     w_copy["dec2a"].wait()
 
@@ -429,8 +465,8 @@
     @pl.when(go)
     def _():
         put("e2", act(conv_sum("u2", "dec2a", 0, 768, 1) + acc2[...].reshape(576, 384), "dec2a"), 1)
-
-    clear_outside("e2")
+        clear_outside("e2")
+
     w_copy["dec2b"].wait()
 
     @pl.when(go)
@@ -438,11 +474,12 @@
         d2[...] = act(conv_sum("e2", "dec2b", 0, 384), "dec2b")
 
     up(d2, "up1", "u1")
-    send("u1")
-
-    @pl.when(go)
-    def _():
-        acc1[...] = acc1[...] + conv_sum("u1", "dec1a", 0, 384, 1).reshape(acc1.shape)
+    launch("u1")
+
+    @pl.when(go)
+    def _():
+        late = conv_sum("u1", "dec1a", 0, 384, 1) + conv_sum("s1", "dec1a", 192, 384, 1, range(6, 9))
+        acc1[...] = acc1[...] + late.reshape(acc1.shape)
 
     settle(SHARED[:-1])
     receive("u1")
@@ -450,12 +487,9 @@
     @pl.when(go)
     def _():
         ring_sum("u1", "dec1a", 0, 384, acc1)
-
-    @pl.when(go)
-    def _():
         put("e1", act(acc1[...].reshape(1600, 192), "dec1a"), 1)
-
-    clear_outside("e1")
+        clear_outside("e1")
+
     w_copy["dec1b"].wait()
 
     @pl.when(go)
@@ -503,7 +537,7 @@
         scratch += [pltpu.VMEM((4, 8, MAPS[n][2]), BF) for n in SHARED] * 2
         scratch += [pltpu.VMEM((10, 10, 16, 128), BF), pltpu.VMEM((128, 192), F32), pltpu.VMEM((64, 768), BF),
                     pltpu.VMEM((256, 384), BF), pltpu.VMEM((1024, 192), BF), pltpu.VMEM((10, 10, 16, 192), F32),
-                    pltpu.VMEM((6, 6, 16, 384), F32), pltpu.VMEM((out_channels, 8, 128), F32)]
+                    pltpu.VMEM((6, 6, 16, 384), F32), pltpu.VMEM((8, 8, 16, 192), F32), pltpu.VMEM((out_channels, 8, 128), F32)]
         scratch += [pltpu.SemaphoreType.DMA((len(SMALL),)), pltpu.SemaphoreType.DMA((len(WEIGHTS),)), pltpu.SemaphoreType.DMA((len(SHARED), 8)),
                     pltpu.SemaphoreType.DMA((len(SHARED), 8))]
         y = pl.pallas_call(

time: 42.2 us -> 41.2 us (0.976)
  Pallas kernels: 40.5 us -> 39.5 us
    pallas_call x1, Pallas kernels: 40.5 us -> 39.5 us  [device_body(): pl.pallas_call(functools.partial(body, rows, cols), out_shape=jax.ShapeDt...]
where the time goes in v5:
time: 41.2 us; the launch traced here: 41.1 us
  Pallas kernels  39.5 us (96%)
  local copies, waits for them, and re-layouts  1.54 us (4%)
    pallas_call x1, Pallas kernels, device_body(): pl.pallas_call(functools.partial(body, rows, cols), out_shape=jax.ShapeDt...  39.5 us
    unnamed x1, local copies, waits for them, and re-layouts  1.54 us

profile of v5, /device:TPU:97, one launch (start us, length us, event | category | flops | bytes accessed | tf_op | source)
XLA Modules:
  0.0 41.1 jit_solution(8998557866134236144)
XLA Ops:
  0.0 39.5 %unet.1 = f32[6,32,32]{2,1,0:T(8,128)} custom-call(f32[6]{0:T(128)} %refs_0_.1, bf16[3,32,32]{2,1,0:T(8,128)(2,1)} %bitcast.31, bf16[9,3,192]{2,1,0:T(4,128)(2,1)} %bitcast.32, bf16[6,192]{1,0:T(8,128)(2,1)} %bitcast.33, f32[192]{0:T(256)} %refs_4_.1, f32[192]{0:T(256)} %refs_5_.1, f32[384]{0:T(512)} %refs_6_.1, f32[384]{0:T(512)} %refs_7_.1, f32[768]{0:T(1024)} %refs_8_.1, ...), custom_call_target="tpu_custom_call" | custom-call | tf_op jit(solution)/shard_map/unet/pallas_call | solution.py:543
  39.5 1.5 %copy.27 = f32[32,32,6]{1,0,2:T(8,128)} copy(f32[32,32,6]{1,0,2:T(8,128)} %bitcast.30) | data formatting | bytes 49152

commit v6 on v5

--- a/solution.py
+++ b/solution.py
@@ -346,9 +346,6 @@
     z = jnp.dot(z.T.astype(BF), jnp.where(spread, 1.0, 0.0).astype(BF), preferred_element_type=F32).astype(BF)
     for hl in range(8):
         maps["x"][2 + hl, 2:10] = z[:, 128 * hl:128 * hl + 128].reshape(8, 16, 128)
-    w27[...] = jnp.zeros(w27.shape, F32)
-    for t in range(9):
-        w27[pl.ds(3 * t, 3), :] = w_enc1a[t].astype(F32)
 
     pl.semaphore_wait(barrier, count)
     def lanes_of(value, shift):
@@ -370,6 +367,9 @@
         return act(jnp.dot(value.reshape(-1, 128), w27[...].astype(BF), preferred_element_type=F32), "enc1a").reshape(-1, 16, 192)
 
     send("x")
+    w27[...] = jnp.zeros(w27.shape, F32)
+    for t in range(9):
+        w27[pl.ds(3 * t, 3), :] = w_enc1a[t].astype(F32)
     patches(range(2, 8), range(2, 8))
     clear_ring("u1")
     clear_ring("p1")
@@ -440,7 +440,7 @@
 
     @pl.when(go)
     def _():
-        acc1[...] = conv_sum("s1", "dec1a", 192, 384, 1, range(6)).reshape(acc1.shape)
+        acc1[...] = conv_sum("s1", "dec1a", 192, 384, 1, range(7)).reshape(acc1.shape)
 
     receive("p2")
     launch("s2")
@@ -478,7 +478,7 @@
 
     @pl.when(go)
     def _():
-        late = conv_sum("u1", "dec1a", 0, 384, 1) + conv_sum("s1", "dec1a", 192, 384, 1, range(6, 9))
+        late = conv_sum("u1", "dec1a", 0, 384, 1) + conv_sum("s1", "dec1a", 192, 384, 1, range(7, 9))
         acc1[...] = acc1[...] + late.reshape(acc1.shape)
 
     settle(SHARED[:-1])

time: 41.2 us -> 41.2 us (level)
  no operation moved by 1% of the time
where the time goes in v6:
time: 41.2 us; the launch traced here: 41.1 us
  Pallas kernels  39.5 us (96%)
  local copies, waits for them, and re-layouts  1.54 us (4%)
    pallas_call x1, Pallas kernels, device_body(): pl.pallas_call(functools.partial(body, rows, cols), out_shape=jax.ShapeDt...  39.5 us
    unnamed x1, local copies, waits for them, and re-layouts  1.54 us

profile of v6, /device:TPU:97, one launch (start us, length us, event | category | flops | bytes accessed | tf_op | source)
XLA Modules:
  0.0 41.1 jit_solution(1925829790563621599)
XLA Ops:
  0.0 39.5 %unet.1 = f32[6,32,32]{2,1,0:T(8,128)} custom-call(f32[6]{0:T(128)} %refs_0_.1, bf16[3,32,32]{2,1,0:T(8,128)(2,1)} %bitcast.31, bf16[9,3,192]{2,1,0:T(4,128)(2,1)} %bitcast.32, bf16[6,192]{1,0:T(8,128)(2,1)} %bitcast.33, f32[192]{0:T(256)} %refs_4_.1, f32[192]{0:T(256)} %refs_5_.1, f32[384]{0:T(512)} %refs_6_.1, f32[384]{0:T(512)} %refs_7_.1, f32[768]{0:T(1024)} %refs_8_.1, ...), custom_call_target="tpu_custom_call" | custom-call | tf_op jit(solution)/shard_map/unet/pallas_call | solution.py:543
  39.5 1.5 %copy.27 = f32[32,32,6]{1,0,2:T(8,128)} copy(f32[32,32,6]{1,0,2:T(8,128)} %bitcast.30) | data formatting | bytes 49152
